TPU v7x, 32 devices: a whole 2x2x4 slice. The times are simulated.
32 devices in a mesh: dp: 4 (over y, x), row: 4 (over z), col: 2 (over core).
Axes of the slice: x: 2, y: 2, z: 4, core: 2. Of those that a mesh axis runs over, the one named last changes fastest.
Arguments:
- block_input: bfloat16 [192, 197, 384], P(('dp', 'row', 'col')), may hold values from -6 to 6
- first_norm_scale: float32 [384], P('row'), may hold values from 0.5 to 1.5
- first_norm_bias: float32 [384], P('row'), may hold values from -1.5 to 1.5
- attn_weight: bfloat16 [6, 384, 256], P('col', 'row'), may hold values from -1.2247449 to 1.2247449
- qv_bias: float32 [2, 384], P(None, 'col'), may hold values from -2.5 to 2.5
- out_bias: float32 [384], P('row'), may hold values from -2.5 to 2.5
- second_norm_scale: float32 [384], P('row'), may hold values from 0.5 to 1.5
- second_norm_bias: float32 [384], P('row'), may hold values from -1.5 to 1.5
- up_weight: bfloat16 [384, 1536], P('row', 'col'), may hold values from -0.3125 to 0.3125
- up_bias: float32 [1536], P('col'), may hold values from -2.5 to 2.5
- down_weight: bfloat16 [384, 1536], P('row', 'col'), may hold values from -0.15625 to 0.15625
- down_bias: float32 [384], P('row'), may hold values from -2.5 to 2.5
- cotangent: bfloat16 [192, 197, 384], P(('dp', 'row', 'col')), may hold values from -6 to 6
Outputs:
- block_output: bfloat16 [192, 197, 384], P(('dp', 'row', 'col'))
- d_x: float32 [192, 197, 384], P(('dp', 'row', 'col'))
- d_ln1_gain: float32 [384], P('row')
- d_ln1_shift: float32 [384], P('row')
- d_attn_weight: float32 [6, 384, 256], P('col', 'row')
- d_qv_bias: float32 [2, 384], P(None, 'col')
- d_out_bias: float32 [384], P('row')
- d_ln2_gain: float32 [384], P('row')
- d_ln2_shift: float32 [384], P('row')
- d_up_weight: float32 [384, 1536], P('row', 'col')
- d_up_bias: float32 [1536], P('col')
- d_down_weight: float32 [384, 1536], P('row', 'col')
- d_down_bias: float32 [384], P('row')
All inputs are finite; a program needn't handle non-finite values.
Results may differ from a plain program's by a relative error of at most 0.013.
Values may be sent and summed in bfloat16 or wider, within the bound.
A program may use at most 448 MiB of HBM per device.

v0:
```python
import math
import jax
import jax.numpy as jnp
from jax import lax
from jax.sharding import PartitionSpec as P

SEQ = 197
HD = 64
EPS = 1e-06
ROOT_HALF = 0.7071067811865476
INV_ROOT_TWO_PI = 0.3989422804014327


def gelu_parts(u):
    cdf = 0.5 * (1.0 + jax.scipy.special.erf(u * ROOT_HALF))
    return (u * cdf, cdf + u * jnp.exp(-0.5 * u * u) * INV_ROOT_TWO_PI)


def row_sum_values(pair):
    return lax.psum((pair[0], pair[1]), "row")


def layer_norm_forward(input_value, scale_factor, offset_bias, feature_width):
    partial_sum_values = row_sum_values(
        (jnp.sum(input_value, -1), jnp.sum(input_value * input_value, -1))
    )
    row_average = partial_sum_values[0] / feature_width
    var = partial_sum_values[1] / feature_width - row_average * row_average
    inverse_deviation = lax.rsqrt(var + EPS)[..., None]
    normalized_input = (input_value - row_average[..., None]) * inverse_deviation
    return (
        normalized_input,
        inverse_deviation,
        (normalized_input * scale_factor + offset_bias).astype(jnp.bfloat16),
    )


def layer_norm_backward(
    incoming_gradient, normalized_input, inverse_deviation, scale_factor, feature_width
):
    normalized_gradient = incoming_gradient * scale_factor
    partial_sum_values = row_sum_values(
        (jnp.sum(normalized_gradient, -1), jnp.sum(normalized_gradient * normalized_input, -1))
    )
    return inverse_deviation * (
        normalized_gradient
        - partial_sum_values[0][..., None] / feature_width
        - normalized_input * (partial_sum_values[1][..., None] / feature_width)
    )


def gather_cols(values):
    return lax.all_gather(values, "col", axis=0, tiled=True)


def gather_rows(values):
    return lax.all_gather(values, "row", axis=0, tiled=True)


def project_in(whole_rows, weight):
    mine = lax.all_to_all(whole_rows, "row", split_axis=0, concat_axis=2, tiled=True)
    full_weight = lax.all_gather(weight, "row", axis=0, tiled=True)
    return jnp.dot(mine, full_weight, preferred_element_type=jnp.float32)


def project_out(whole_rows, weight):
    return lax.psum_scatter(
        jnp.dot(whole_rows, weight, preferred_element_type=jnp.float32),
        "col",
        scatter_dimension=0,
        tiled=True,
    )


def back_to_middle(whole_grad, weight):
    mine = lax.all_to_all(whole_grad, "row", split_axis=0, concat_axis=2, tiled=True)
    full_weight = lax.all_gather(weight, "row", axis=1, tiled=True)
    return lax.dot_general(
        mine, full_weight, (((2,), (1,)), ((), ())), preferred_element_type=jnp.float32
    )


def back_to_input(whole_grad, weight):
    return lax.psum_scatter(
        lax.dot_general(
            whole_grad, weight, (((2,), (1,)), ((), ())), preferred_element_type=jnp.float32
        ),
        "col",
        scatter_dimension=0,
        tiled=True,
    )


def token_product(left, incoming_gradient):
    return lax.dot_general(
        left, incoming_gradient, (((0, 1), (0, 1)), ((), ())), preferred_element_type=jnp.float32
    )


def token_sum(incoming_gradient):
    return jnp.sum(incoming_gradient, axis=(0, 1), dtype=jnp.float32)


def sum_weights(grads):
    return (
        lax.psum(grads[0].astype(jnp.bfloat16), "dp").astype(jnp.float32),
        lax.psum(grads[1].astype(jnp.bfloat16), "dp").astype(jnp.float32),
        lax.psum(grads[2].astype(jnp.bfloat16), "dp").astype(jnp.float32),
        lax.psum(grads[3].astype(jnp.bfloat16), "dp").astype(jnp.float32),
        lax.psum(grads[4].astype(jnp.bfloat16), "dp").astype(jnp.float32),
        lax.psum(grads[5].astype(jnp.bfloat16), "dp").astype(jnp.float32),
        lax.psum(grads[6].astype(jnp.bfloat16), "dp").astype(jnp.float32),
    )


def sum_norms(grads):
    return lax.psum((grads[0], grads[1], grads[2], grads[3]), ("dp", "col"))


def attend_block(inputs):
    query, keys, values = inputs
    scale = 1.0 / math.sqrt(query.shape[-1])
    scores = jnp.einsum("bqhd,bkhd->bhqk", query, keys, preferred_element_type=jnp.float32) * scale
    top = jnp.max(scores, -1, keepdims=True)
    lse = top + jnp.log(jnp.sum(jnp.exp(scores - top), -1, keepdims=True))
    probs = jnp.exp(scores - lse).astype(jnp.bfloat16)
    out = jnp.einsum("bhqk,bkhd->bqhd", probs, values, preferred_element_type=jnp.float32)
    return (out.astype(jnp.bfloat16), lse)


def attend_back_block(inputs):
    query, keys, values, lse, dout = inputs
    scale = 1.0 / math.sqrt(query.shape[-1])
    scores = jnp.einsum("bqhd,bkhd->bhqk", query, keys, preferred_element_type=jnp.float32) * scale
    probs = jnp.exp(scores - lse)
    probs_b = probs.astype(jnp.bfloat16)
    dvals = jnp.einsum("bhqk,bqhd->bkhd", probs_b, dout, preferred_element_type=jnp.float32)
    dprob = jnp.einsum("bqhd,bkhd->bhqk", dout, values, preferred_element_type=jnp.float32)
    delta = jnp.sum(probs * dprob, -1, keepdims=True)
    dsb = (probs * (dprob - delta)).astype(jnp.bfloat16)
    dquery = jnp.einsum("bhqk,bkhd->bqhd", dsb, keys, preferred_element_type=jnp.float32) * scale
    dkeys = jnp.einsum("bhqk,bqhd->bkhd", dsb, query, preferred_element_type=jnp.float32) * scale
    return (dquery.astype(jnp.bfloat16), dkeys.astype(jnp.bfloat16), dvals.astype(jnp.bfloat16))


def local(
    block_input,
    first_norm_scale,
    first_norm_bias,
    attn_weight,
    qv_bias,
    out_bias,
    second_norm_scale,
    second_norm_bias,
    up_weight,
    up_bias,
    down_weight,
    down_bias,
    cotangent,
):
    split_input, split_cotangent = (
        lax.all_to_all(block_input, "row", split_axis=2, concat_axis=0, tiled=True),
        lax.all_to_all(cotangent, "row", split_axis=2, concat_axis=0, tiled=True),
    )
    head_count = attn_weight.shape[0]
    feat_rows = attn_weight.shape[1]
    feat_cols = head_count * HD
    feature_width = feat_rows * lax.axis_size("row")
    qkv_local = (
        attn_weight[:, :, : 3 * HD]
        .reshape(head_count, feat_rows, 3, HD)
        .transpose(1, 2, 0, 3)
        .reshape(feat_rows, 3 * feat_cols)
    )
    out_local = attn_weight[:, :, 3 * HD :].transpose(0, 2, 1).reshape(feat_cols, feat_rows)
    down_local = down_weight.T
    input_as_float = split_input.astype(jnp.float32)
    first_normalized_input, first_inverse_deviation, first_normed_output = layer_norm_forward(
        input_as_float, first_norm_scale, first_norm_bias, feature_width
    )
    whole1 = gather_cols(first_normed_output)
    qkv = project_in(whole1, qkv_local)
    images_mine = qkv.shape[0]
    bias_three = jnp.stack([qv_bias[0], jnp.zeros_like(qv_bias[0]), qv_bias[1]])
    qkv = qkv.reshape(images_mine, SEQ, 3, feat_cols) + bias_three
    group = math.gcd(images_mine, 6)
    nblocks = images_mine // group
    split_shape = (nblocks, group, SEQ, head_count, HD)
    query = qkv[:, :, 0].astype(jnp.bfloat16).reshape(split_shape)
    keys = qkv[:, :, 1].astype(jnp.bfloat16).reshape(split_shape)
    values = qkv[:, :, 2].astype(jnp.bfloat16).reshape(split_shape)
    attn, lse = lax.map(attend_block, (query, keys, values))
    attn_flat = attn.reshape(images_mine, SEQ, feat_cols)
    attn_whole = gather_rows(attn_flat)
    hidden_input = input_as_float + project_out(attn_whole, out_local) + out_bias
    second_normalized_input, second_inverse_deviation, second_normed_output = layer_norm_forward(
        hidden_input, second_norm_scale, second_norm_bias, feature_width
    )
    whole2 = gather_cols(second_normed_output)
    pre = project_in(whole2, up_weight) + up_bias
    act, slope = gelu_parts(pre)
    act_b = act.astype(jnp.bfloat16)
    act_whole = gather_rows(act_b)
    y_out = (hidden_input + project_out(act_whole, down_local) + down_bias).astype(jnp.bfloat16)
    grad_whole = gather_cols(split_cotangent)
    g_down_w = token_product(grad_whole, act_whole)
    g_down_b = token_sum(grad_whole)
    dpre = (back_to_middle(grad_whole, down_local) * slope).astype(jnp.bfloat16)
    dpre_whole = gather_rows(dpre)
    g_up_w = token_product(whole2, dpre_whole)
    g_up_b = token_sum(dpre_whole)
    second_activation_grad = back_to_input(dpre_whole, up_weight)
    second_norm_scale_grad = jnp.sum(second_activation_grad * second_normalized_input, (0, 1))
    g_ln2_s = jnp.sum(second_activation_grad, (0, 1))
    hidden_gradient = split_cotangent.astype(jnp.float32) + layer_norm_backward(
        second_activation_grad,
        second_normalized_input,
        second_inverse_deviation,
        second_norm_scale,
        feature_width,
    )
    dhb = hidden_gradient.astype(jnp.bfloat16)
    dh_whole = gather_cols(dhb)
    g_out_w = token_product(attn_whole, dh_whole)
    g_out_b = token_sum(dh_whole)
    dout = back_to_middle(dh_whole, out_local).astype(jnp.bfloat16).reshape(split_shape)
    dquery, dkeys, dvals = lax.map(attend_back_block, (query, keys, values, lse, dout))
    dqkv = jnp.stack(
        [
            dquery.reshape(images_mine, SEQ, feat_cols),
            dkeys.reshape(images_mine, SEQ, feat_cols),
            dvals.reshape(images_mine, SEQ, feat_cols),
        ],
        2,
    ).reshape(images_mine, SEQ, 3 * feat_cols)
    dqkv_whole = gather_rows(dqkv)
    g_qkv_w = token_product(whole1, dqkv_whole)
    bias_sums = token_sum(dqkv_whole).reshape(3, feat_cols)
    g_qv_b = jnp.stack([bias_sums[0], bias_sums[2]])
    packed_qkv = (
        g_qkv_w.reshape(feat_rows, 3, head_count, HD)
        .transpose(2, 0, 1, 3)
        .reshape(head_count, feat_rows, 3 * HD)
    )
    packed_out = g_out_w.reshape(head_count, HD, feat_rows).transpose(0, 2, 1)
    g_attn = jnp.concatenate([packed_qkv, packed_out], 2)
    first_activation_grad = back_to_input(dqkv_whole, qkv_local)
    first_norm_scale_grad = jnp.sum(first_activation_grad * first_normalized_input, (0, 1))
    g_ln1_s = jnp.sum(first_activation_grad, (0, 1))
    output_input_gradient = hidden_gradient + layer_norm_backward(
        first_activation_grad,
        first_normalized_input,
        first_inverse_deviation,
        first_norm_scale,
        feature_width,
    )
    totals = sum_weights((g_attn, g_qv_b, g_out_b, g_up_w, g_up_b, g_down_w, g_down_b))
    norms = sum_norms((first_norm_scale_grad, g_ln1_s, second_norm_scale_grad, g_ln2_s))
    y_back, dx_back = (
        lax.all_to_all(
            y_out.astype(jnp.float32).astype(jnp.bfloat16),
            "row",
            split_axis=0,
            concat_axis=2,
            tiled=True,
        ).astype(jnp.float32),
        lax.all_to_all(
            output_input_gradient.astype(jnp.bfloat16),
            "row",
            split_axis=0,
            concat_axis=2,
            tiled=True,
        ).astype(output_input_gradient.dtype),
    )
    return (
        y_back.astype(jnp.bfloat16),
        dx_back,
        norms[0],
        norms[1],
        totals[0],
        totals[1],
        totals[2],
        norms[2],
        norms[3],
        totals[3],
        totals[4],
        totals[5],
        totals[6],
    )


def solution(mesh):
    placed = (
        P(("dp", "row", "col"), None, None),
        P("row"),
        P("row"),
        P("col", "row", None),
        P(None, "col"),
        P("row"),
        P("row"),
        P("row"),
        P("row", "col"),
        P("col"),
        P("row", "col"),
        P("row"),
        P(("dp", "row", "col"), None, None),
    )
    return jax.shard_map(
        local,
        mesh=mesh,
        in_specs=placed,
        out_specs=(
            P(("dp", "row", "col"), None, None),
            P(("dp", "row", "col"), None, None),
            P("row"),
            P("row"),
            P("col", "row", None),
            P(None, "col"),
            P("row"),
            P("row"),
            P("row"),
            P("row", "col"),
            P("col"),
            P("row", "col"),
            P("row"),
        ),
        check_vma=False,
    )
```

profile of v0, /device:TPU:0, one launch (start us, length us, event | category | flops | bytes accessed | tf_op | source)
XLA Modules:
  0.0 1588.9 jit_solution(12312043903524667726)
XLA Ops:
  9.5 43.1 %all_to_all.126 = bf16[6,197,384]{1,0,2:T(8,128)(2,1)S(1)} all-to-all(bf16[6,197,384]{1,0,2:T(8,128)(2,1)S(1)} %copy.109), channel_id=1, replica_groups=mesh['dp'=4,'row'=4,'col'=2] {'row'}, dimensions={2} | all-to-all | bytes 1815552 | tf_op jit(solution)/shard_map/all_to_all | solution.py:162
  62.7 17.6 %all-reduce.4 = (f32[24,197]{1,0:T(8,128)S(1)}, f32[24,197]{1,0:T(8,128)S(1)}) all-reduce(f32[24,197]{1,0:T(8,128)S(1)} %reduce_sum.178, f32[24,197]{1,0:T(8,128)S(1)} %reduce_sum.176), channel_id=1, replica_groups=mesh['dp'=4,'row'=4,'col'=2] {'row'}, use_global_device_ids=true, to_apply=%region_3.0 | all-reduce | flops 9456 | bytes 75648 | tf_op jit(solution)/shard_map/psum | solution.py:20
  82.5 9.3 all-gather.9.cloned.1.call-done
  91.9 4.9 all-to-all-start.1
  97.8 63.3 %all_gather.37 = bf16[384,576]{1,0:T(8,128)(2,1)S(1)} all-gather(bf16[96,576]{1,0:T(8,128)(2,1)S(1)} %copy.117), channel_id=1, replica_groups=mesh['dp'=4,'row'=4,'col'=2] {'row'}, dimensions={0}, use_global_device_ids=true | all-gather | bytes 552960 | tf_op jit(solution)/shard_map/all_gather | solution.py:62
  176.2 7.9 while.26
  187.2 80.7 %all_to_all.127 = bf16[6,197,384]{1,0,2:T(8,128)(2,1)} all-to-all(bf16[6,197,384]{1,0,2:T(8,128)(2,1)} %copy.123), channel_id=1, replica_groups=mesh['dp'=4,'row'=4,'col'=2] {'row'}, dimensions={2} | all-to-all | bytes 1815552 | tf_op jit(solution)/shard_map/all_to_all | solution.py:163
  277.8 24.4 %all-gather.11.cloned.1.call-done = bf16[48,197,192]{1,2,0:T(8,128)(2,1)} async-done(((bf16[12,197,192]{1,2,0:T(8,128)(2,1)}), bf16[48,197,192]{1,2,0:T(8,128)(2,1)}) %all-gather.11.cloned.1.call-update) | async-done | bytes 3631120 | tf_op jit(solution)/shard_map/all_gather | solution.py:57
  302.3 5.3 fusion.86
  307.6 6.2 all-gather.17.cloned.1.call-done
  313.8 4.9 all-to-all-start.5
  318.7 11.0 reduce-scatter.5.cloned.1.call-done
  329.7 5.1 fusion.81
  334.9 48.0 %all-reduce.3 = (f32[24,197]{1,0:T(8,128)}, f32[24,197]{1,0:T(8,128)}) all-reduce(f32[24,197]{1,0:T(8,128)} %get-tuple-element.150, f32[24,197]{1,0:T(8,128)} %get-tuple-element.149), channel_id=1, replica_groups=mesh['dp'=4,'row'=4,'col'=2] {'row'}, use_global_device_ids=true, to_apply=%region_12.13 | all-reduce | flops 9456 | bytes 75648 | tf_op jit(solution)/shard_map/psum | solution.py:20
  387.5 11.2 all-gather.13.cloned.1.call-done
  398.7 4.9 all-to-all-start.2
  403.6 65.9 %all_gather.43 = bf16[768,384]{0,1:T(8,128)(2,1)} all-gather(bf16[768,96]{0,1:T(8,128)(2,1)} %bitcast.266), channel_id=1, replica_groups=mesh['dp'=4,'row'=4,'col'=2] {'row'}, dimensions={1}, use_global_device_ids=true | all-gather | bytes 737280 | tf_op jit(solution)/shard_map/all_gather | solution.py:77
  469.5 17.0 %all_gather.40 = bf16[384,768]{1,0:T(8,128)(2,1)} all-gather(bf16[96,768]{1,0:T(8,128)(2,1)} %param.25), channel_id=1, replica_groups=mesh['dp'=4,'row'=4,'col'=2] {'row'}, dimensions={0}, use_global_device_ids=true | all-gather | bytes 737280 | tf_op jit(solution)/shard_map/all_gather | solution.py:62
  486.5 5.5 copy.126
  491.9 5.3 all_to_all.112
  497.3 5.5 copy.121
  502.8 5.3 all_to_all.100
  508.1 5.5 multiply_convert_fusion.1
  518.5 254.0 %all-gather.19.cloned.1.call-done = bf16[48,197,768]{2,1,0:T(8,128)(2,1)} async-done(((bf16[12,197,768]{2,1,0:T(8,128)(2,1)}), bf16[48,197,768]{2,1,0:T(8,128)(2,1)}) %all-gather.19.cloned.1.call-update) | async-done | bytes 14524432 | tf_op jit(solution)/shard_map/all_gather | solution.py:57
  772.5 9.5 fusion.76
  782.1 10.8 reduce-scatter.9.cloned.1.call-done
  797.0 21.1 %all-reduce.2 = (f32[24,197]{1,0:T(8,128)}, f32[24,197]{1,0:T(8,128)}) all-reduce(f32[24,197]{1,0:T(8,128)} %get-tuple-element.140, f32[24,197]{1,0:T(8,128)} %get-tuple-element.146), channel_id=1, replica_groups=mesh['dp'=4,'row'=4,'col'=2] {'row'}, use_global_device_ids=true, to_apply=%region_18.19 | all-reduce | flops 9456 | bytes 75648 | tf_op jit(solution)/shard_map/psum | solution.py:20
  824.2 9.3 all-gather.21.cloned.1.call-done
  833.5 4.9 all-to-all-start.6
  839.9 60.5 %all_gather.46 = bf16[192,384]{0,1:T(8,128)(2,1)} all-gather(bf16[192,96]{0,1:T(8,128)(2,1)} %copy.128), channel_id=1, replica_groups=mesh['dp'=4,'row'=4,'col'=2] {'row'}, dimensions={1}, use_global_device_ids=true | all-gather | bytes 184320 | tf_op jit(solution)/shard_map/all_gather | solution.py:77
  900.4 5.5 copy.127
  905.9 5.3 all_to_all.116
  918.1 17.9 %while.27 = (s32[]{:T(128)}, bf16[2,6,197,3,64]{2,4,3,1,0:T(8,128)(2,1)}, bf16[2,6,197,3,64]{2,4,3,1,0:T(8,128)(2,1)}, bf16[2,6,197,3,64]{2,4,3,1,0:T(8,128)(2,1...) while((s32[]{:T(128)}, ...), condition=%wide.region_21.22_spmd, body=%wide.region_19.21_spmd.sunk | while | flops 456593600 | bytes 55074784 | solution.py:227
  942.8 213.1 %all-gather.23.cloned.1.call-done = bf16[48,197,576]{2,1,0:T(8,128)(2,1)} async-done(((bf16[12,197,576]{2,1,0:T(8,128)(2,1)}), bf16[48,197,576]{2,1,0:T(8,128)(2,1)}) %all-gather.23.cloned.1.call-update) | async-done | bytes 10893328 | tf_op jit(solution)/shard_map/all_gather | solution.py:57
  1155.9 11.7 fusion.87
  1168.0 241.0 %all-gather.15.cloned.1.call-done = bf16[48,197,768]{2,1,0:T(8,128)(2,1)} async-done(((bf16[12,197,768]{2,1,0:T(8,128)(2,1)}), bf16[48,197,768]{2,1,0:T(8,128)(2,1)}) %all-gather.15.cloned.1.call-update) | async-done | bytes 14524432 | tf_op jit(solution)/shard_map/all_gather | solution.py:57
  1409.0 11.9 fusion.78
  1422.8 8.4 fusion.70
  1435.7 18.1 %all-reduce.1 = (f32[24,197]{1,0:T(8,128)}, f32[24,197]{1,0:T(8,128)}) all-reduce(f32[24,197]{1,0:T(8,128)} %get-tuple-element.142, f32[24,197]{1,0:T(8,128)} %get-tuple-element.145), channel_id=1, replica_groups=mesh['dp'=4,'row'=4,'col'=2] {'row'}, use_global_device_ids=true, to_apply=%region_26.27 | all-reduce | flops 9456 | bytes 75648 | tf_op jit(solution)/shard_map/psum | solution.py:20
  1456.6 7.5 add_convert_fusion.1
  1467.6 8.1 fusion.67
  1480.0 12.8 all-to-all-done.3
  1497.3 7.1 fusion.69
  1511.3 7.4 reduce_sum.191
  1519.8 6.6 reduce.5
  1526.5 10.1 all-reduce.5
  1538.7 17.3 %all-reduce.9.cloned.1.call-done = (bf16[3,96,256]{1,2,0:T(8,128)(2,1)}, bf16[96,768]{1,0:T(8,128)(2,1)}, bf16[96,768]{1,0:T(8,128)(2,1)}) async-done(((bf16[3,96,256]{1,2,0:T(8,128)(2,1)}, bf16[96,768]{1,0:T(8,128)(2,1)}, bf16[96,768]{1,0:T(8,128)(2,1)}), (bf16[3,96,256]{1,2,0:T(8,128)(2,1)}, bf16[96,768]{1,0:T(8,128)(2,1)}, bf16[96,768]{1,0:T(8,128)(2,1)})) %all-reduce.9.cloned.1.call-update) | async-done | bytes 442384 | tf_op jit(solution)/shard_map/psum | solution.py:106
  1561.1 12.6 all-reduce
  (229 shorter events, 149.6 us)
Async XLA Ops:
  7.2 84.7 %all-gather.9.cloned.1.call-start = ((), (), s32[]{:S(2)}) async-start(), calls=%async_computation.12 | async-start | bytes 3538944 | tf_op jit(solution)/shard_map/all_gather | solution.py:53
  55.3 4.4 copy-start.3
  59.7 21.2 %copy-start.31 = (f32[96]{0:T(128)S(1)}, f32[96]{0:T(128)}, u32[]{:S(2)}) copy-start(f32[96]{0:T(128)} %param.18) | copy-start | bytes 1156
  59.7 21.2 %copy-start.38 = (f32[96]{0:T(128)S(1)}, f32[96]{0:T(128)}, u32[]{:S(2)}) copy-start(f32[96]{0:T(128)} %param.19) | copy-start | bytes 1156
  62.7 19.8 %copy-start.1 = (f32[4,6,197,96]{2,3,1,0:T(8,128)}, f32[4,6,197,96]{2,3,1,0:T(8,128)S(1)}, u32[]{:S(2)}) copy-start(f32[4,6,197,96]{2,3,1,0:T(8,128)S(1)} %copy.111) | copy-start | bytes 5446660
  82.5 14.2 copy-start.25
  91.9 69.6 %all-to-all-start.1 = ((bf16[48,197,96]{1,2,0:T(8,128)(2,1)}), bf16[48,197,96]{1,2,0:T(8,128)(2,1)S(1)}, u32[]{:S(2)}, u32[]{:S(2)}) async-start(bf16[48,197,96]{1,2,0:T(8,128)(2,1)} %all-gather.9.cloned.1.call-done), calls=%async_computation.1 | async-start | bytes 4718592 | tf_op jit(solution)/shard_map/all_to_all | solution.py:61
  96.7 64.6 %copy-start.35 = (f32[2,192]{1,0:T(2,128)S(1)}, f32[2,192]{1,0:T(2,128)}, u32[]{:S(2)}) copy-start(f32[2,192]{1,0:T(2,128)} %param.21) | copy-start | bytes 4612
  96.7 205.5 %all-gather.11.cloned.1.call-start = ((), (), s32[]{:S(2)}) async-start(), calls=%async_computation.13 | async-start | bytes 5898240 | tf_op jit(solution)/shard_map/all_gather | solution.py:57
  161.4 1.5 copy-start.7
  177.0 1.3 copy-start.14
  177.8 1.3 copy-start.27
  181.7 1.3 copy-start.27
  184.1 129.7 %all-gather.17.cloned.1.call-start = ((), (), s32[]{:S(2)}) async-start(), calls=%async_computation.18 | async-start | bytes 3538944 | tf_op jit(solution)/shard_map/all_gather | solution.py:53
  274.6 55.2 %reduce-scatter.5.cloned.1.call-start = ((), (), s32[]{:S(2)}) async-start(), calls=%async_computation.14 | async-start | bytes 7077888 | tf_op jit(solution)/shard_map/reduce_scatter | solution.py:67
  307.6 22.1 %copy-start.39 = (f32[96]{0:T(128)S(1)}, f32[96]{0:T(128)}, u32[]{:S(2)}) copy-start(f32[96]{0:T(128)} %param.22) | copy-start | bytes 1156
  313.8 73.6 %all-to-all-start.5 = ((bf16[48,197,96]{1,2,0:T(8,128)(2,1)}), bf16[48,197,96]{1,2,0:T(8,128)(2,1)}, u32[]{:S(2)}, u32[]{:S(2)}) async-start(bf16[48,197,96]{1,2,0:T(8,128)(2,1)} %all-gather.17.cloned.1.call-done), calls=%async_computation.7 | async-start | bytes 4718592 | tf_op jit(solution)/shard_map/all_to_all | solution.py:76
  318.7 65.5 %copy-start.30 = (f32[96]{0:T(128)S(1)}, f32[96]{0:T(128)}, u32[]{:S(2)}) copy-start(f32[96]{0:T(128)} %param.23) | copy-start | bytes 1156
  318.7 65.5 %copy-start.40 = (f32[96]{0:T(128)S(1)}, f32[96]{0:T(128)}, u32[]{:S(2)}) copy-start(f32[96]{0:T(128)} %param.24) | copy-start | bytes 1156
  318.7 80.0 %all-gather.13.cloned.1.call-start = ((), (), s32[]{:S(2)}) async-start(), calls=%async_computation.15 | async-start | bytes 3538944 | tf_op jit(solution)/shard_map/all_gather | solution.py:53
  398.7 98.6 %all-to-all-start.2 = ((bf16[48,197,96]{1,2,0:T(8,128)(2,1)}), bf16[48,197,96]{1,2,0:T(8,128)(2,1)}, u32[]{:S(2)}, u32[]{:S(2)}) async-start(bf16[48,197,96]{1,2,0:T(8,128)(2,1)} %all-gather.13.cloned.1.call-done), calls=%async_computation.3 | async-start | bytes 4718592 | tf_op jit(solution)/shard_map/all_to_all | solution.py:61
  403.6 368.9 %all-gather.19.cloned.1.call-start = ((), (), s32[]{:S(2)}) async-start(), calls=%async_computation.19 | async-start | bytes 18432000 | tf_op jit(solution)/shard_map/all_gather | solution.py:57
  502.8 5.3 copy-start.41
  508.1 5.5 copy-start.16
  508.1 5.5 copy-start.21
  518.5 274.4 %reduce-scatter.9.cloned.1.call-start = ((), (), s32[]{:S(2)}) async-start(), calls=%async_computation.20 | async-start | bytes 7077888 | tf_op jit(solution)/shard_map/reduce_scatter | solution.py:84
  782.0 51.5 %all-gather.21.cloned.1.call-start = ((), (), s32[]{:S(2)}) async-start(), calls=%async_computation.21 | async-start | bytes 3538944 | tf_op jit(solution)/shard_map/all_gather | solution.py:53
  833.5 66.9 %all-to-all-start.6 = ((bf16[48,197,96]{1,2,0:T(8,128)(2,1)}), bf16[48,197,96]{1,2,0:T(8,128)(2,1)}, u32[]{:S(2)}, u32[]{:S(2)}) async-start(bf16[48,197,96]{1,2,0:T(8,128)(2,1)} %all-gather.21.cloned.1.call-done), calls=%async_computation.9 | async-start | bytes 4718592 | tf_op jit(solution)/shard_map/all_to_all | solution.py:76
  838.4 317.5 %all-gather.23.cloned.1.call-start = ((), (), s32[]{:S(2)}) async-start(), calls=%async_computation.22 | async-start | bytes 15360000 | tf_op jit(solution)/shard_map/all_gather | solution.py:57
  918.9 1.6 copy-start.8
  927.8 1.6 copy-start.8
  942.1 213.7 %copy-start.18 = (bf16[96,3,3,64]{0,3,2,1:T(8,128)(2,1)S(1)}, bf16[96,3,3,64]{0,3,2,1:T(8,128)(2,1)}, u32[]{:S(2)}) copy-start(bf16[96,3,3,64]{0,3,2,1:T(8,128)(2,1)} %copy-done.17) | copy-start | bytes 331780
  942.1 466.9 %all-gather.15.cloned.1.call-start = ((), (), s32[]{:S(2)}) async-start(), calls=%async_computation.16 | async-start | bytes 18432000 | tf_op jit(solution)/shard_map/all_gather | solution.py:57
  942.7 488.5 %reduce-scatter.11.cloned.1.call-start = ((), (), s32[]{:S(2)}) async-start(), calls=%async_computation.23 | async-start | bytes 7077888 | tf_op jit(solution)/shard_map/reduce_scatter | solution.py:84
  1167.5 241.5 %copy-start.22 = (bf16[96,768]{1,0:T(8,128)(2,1)S(1)}, bf16[96,768]{1,0:T(8,128)(2,1)}, u32[]{:S(2)}) copy-start(bf16[96,768]{1,0:T(8,128)(2,1)} %param.27) | copy-start | bytes 442372
  1167.6 289.0 %reduce-scatter.7.cloned.1.call-start = ((), (), s32[]{:S(2)}) async-start(), calls=%async_computation.17 | async-start | bytes 7077888 | tf_op jit(solution)/shard_map/reduce_scatter | solution.py:67
  1421.0 1.8 copy-start.6
  1422.8 8.4 copy-start.32
  1431.2 25.4 %copy-start = (f32[24,197,96]{1,2,0:T(8,128)S(1)}, f32[24,197,96]{1,2,0:T(8,128)}, u32[]{:S(2)}) copy-start(f32[24,197,96]{1,2,0:T(8,128)} %get-tuple-element.202) | copy-start | bytes 5446660
  1431.2 25.4 %copy-start.5 = (bf16[4,6,197,96]{2,3,1,0:T(8,128)(2,1)S(1)}, bf16[4,6,197,96]{2,3,1,0:T(8,128)(2,1)}, u32[]{:S(2)}) copy-start(bf16[4,6,197,96]{2,3,1,0:T(8,128)(2,1)} %copy.125) | copy-start | bytes 2723332
  1464.0 28.8 %all-to-all-start.3 = ((bf16[24,197,96]{1,2,0:T(8,128)(2,1)}), bf16[24,197,96]{1,2,0:T(8,128)(2,1)S(1)}, u32[]{:S(2)}, u32[]{:S(2)}) async-start(bf16[24,197,96]{1,2,0:T(8,128)(2,1)} %get-tuple-element.211), calls=%async_computation.5 | async-start | bytes 2359296 | tf_op jit(solution)/shard_map/all_to_all | solution.py:260
  1467.6 8.1 copy-start.4
  1492.8 84.3 %all-to-all-start.7 = ((bf16[24,197,96]{1,2,0:T(8,128)(2,1)}), bf16[24,197,96]{1,2,0:T(8,128)(2,1)}, u32[]{:S(2)}, u32[]{:S(2)}) async-start(bf16[24,197,96]{1,2,0:T(8,128)(2,1)} %get-tuple-element.210), calls=%async_computation.11 | async-start | bytes 2359296 | tf_op jit(solution)/shard_map/all_to_all | solution.py:267
  1497.1 58.9 %all-reduce.9.cloned.1.call-start = ((), (), s32[]{:S(2)}) async-start(), calls=%async_computation.24 | async-start | bytes 983040 | tf_op jit(solution)/shard_map/psum | solution.py:106
  1519.7 6.7 copy-start.36
  1519.8 6.7 copy-start.37
  1519.8 41.3 %copy-start.33 = (f32[96]{0:T(128)S(1)}, f32[96]{0:T(128)}, u32[]{:S(2)}) copy-start(f32[96]{0:T(128)} %get-tuple-element.141) | copy-start | bytes 1156
  1519.8 41.3 %copy-start.34 = (f32[96]{0:T(128)S(1)}, f32[96]{0:T(128)}, u32[]{:S(2)}) copy-start(f32[96]{0:T(128)} %get-tuple-element.148) | copy-start | bytes 1156
  (24 other events, 23.4 us)
Sparse Core Ops, SparseCore 0:
  82.6 9.1 all-gather.8
  184.2 117.9 all-gather.10
  303.8 9.9 all-gather.16
  316.0 13.7 reduce-scatter.4
  387.6 11.0 all-gather.12
  518.6 253.8 all-gather.18
  782.1 10.7 reduce-scatter.8
  824.3 9.1 all-gather.20
  942.2 213.5 all-gather.22
  1157.3 251.7 all-gather.14
  1411.3 10.7 reduce-scatter.10
  1424.3 13.8 reduce-scatter.6
  1508.7 47.2 all-reduce.8
where the time goes:
time: 1600 us; the launch traced here: 1590 us
  waiting for transfers between devices  821 us (51%)
  blocking collectives  458 us (29%)
  local copies, waits for them, and re-layouts  104 us (6%)
  matrix products  94.4 us (6%)
  other arithmetic  68 us (4%)
  starting transfers between devices  28.4 us (2%)
    all_gather x4, waiting for transfers between devices, gather_rows(): return lax.all_gather(values, 'row', axis=0, tiled=True)  732 us
    all_gather x2, blocking collectives, back_to_middle(): full_weight = lax.all_gather(weight, 'row', axis=1, tiled=True)  126 us
    psum x4, blocking collectives, row_sum_values(): return lax.psum((pair[0], pair[1]), 'row')  105 us
    all_to_all x1, blocking collectives, local(): lax.all_to_all(cotangent, 'row', split_axis=2, concat_axis=0, tiled=True)  80.7 us
    all_gather x2, blocking collectives, project_in(): full_weight = lax.all_gather(weight, 'row', axis=0, tiled=True)  80.3 us
    all_to_all x1, blocking collectives, local(): lax.all_to_all(block_input, 'row', split_axis=2, concat_axis=0, tiled=True)  43.1 us
    all_gather x4, waiting for transfers between devices, gather_cols(): return lax.all_gather(values, 'col', axis=0, tiled=True)  36.1 us
  transfers between devices with their start and end apart: 19, of which 12 were waited for; matrix products, arithmetic and copies ran while one was open for 8% of the time, Pallas kernels for 0%

commit v1 on v0

--- a/solution.py
+++ b/solution.py
@@ -9,6 +9,17 @@
 EPS = 1e-06
 ROOT_HALF = 0.7071067811865476
 INV_ROOT_TWO_PI = 0.3989422804014327
+
+
+def collect(x, axis, dim):
+    ways = lax.axis_size(axis)
+    pieces = [x]
+    for far in range(1, ways):
+        pieces.append(
+            lax.ppermute(pieces[far - 1], axis, [(d, (d - 1) % ways) for d in range(ways)])
+        )
+    line = jnp.concatenate(pieces, axis=dim)
+    return jnp.roll(line, lax.axis_index(axis) * x.shape[dim], axis=dim)
 
 
 def gelu_parts(u):
@@ -59,7 +70,7 @@
 
 def project_in(whole_rows, weight):
     mine = lax.all_to_all(whole_rows, "row", split_axis=0, concat_axis=2, tiled=True)
-    full_weight = lax.all_gather(weight, "row", axis=0, tiled=True)
+    full_weight = collect(weight, "row", 0)
     return jnp.dot(mine, full_weight, preferred_element_type=jnp.float32)
 
 

time: 1600 us -> 1600 us (level)
  blocking collectives: 458 us -> 340 us
  waiting for transfers between devices: 821 us -> 921 us
  starting transfers between devices: 28.4 us -> 48 us
    ppermute x0 -> x6, waiting for transfers between devices: none -> 98.1 us  [collect(): lax.ppermute(pieces[far - 1], axis, [(d, (d - 1) % ways) for d in range(w...]
    all_gather x2 -> x0, blocking collectives: 80.3 us -> none  [project_in(): full_weight = lax.all_gather(weight, 'row', axis=0, tiled=True)]
    all_gather x2, blocking collectives: 126 us -> 88.2 us  [back_to_middle(): full_weight = lax.all_gather(weight, 'row', axis=1, tiled=True)]
    ppermute x0 -> x6, starting transfers between devices: none -> 19.9 us  [collect(): lax.ppermute(pieces[far - 1], axis, [(d, (d - 1) % ways) for d in range(w...]
  transfers between devices with their start and end apart: 19 -> 25, of which waited for: 12 -> 17; matrix products, arithmetic and copies ran while one was open for 8% -> 8% of each run, Pallas kernels for 0% -> 0%
where the time goes in v1:
time: 1600 us; the launch traced here: 1590 us
  waiting for transfers between devices  921 us (58%)
  blocking collectives  340 us (21%)
  local copies, waits for them, and re-layouts  109 us (7%)
  matrix products  94.5 us (6%)
  other arithmetic  68 us (4%)
  starting transfers between devices  48 us (3%)
    all_gather x4, waiting for transfers between devices, gather_rows(): return lax.all_gather(values, 'row', axis=0, tiled=True)  734 us
    psum x4, blocking collectives, row_sum_values(): return lax.psum((pair[0], pair[1]), 'row')  105 us
    ppermute x6, waiting for transfers between devices, collect(): lax.ppermute(pieces[far - 1], axis, [(d, (d - 1) % ways) for d in range(w...  98.1 us
    all_gather x2, blocking collectives, back_to_middle(): full_weight = lax.all_gather(weight, 'row', axis=1, tiled=True)  88.2 us
    all_to_all x1, blocking collectives, local(): lax.all_to_all(cotangent, 'row', split_axis=2, concat_axis=0, tiled=True)  81.2 us
    all_to_all x1, blocking collectives, local(): lax.all_to_all(block_input, 'row', split_axis=2, concat_axis=0, tiled=True)  43.1 us
    all_gather x4, waiting for transfers between devices, gather_cols(): return lax.all_gather(values, 'col', axis=0, tiled=True)  36.1 us
  transfers between devices with their start and end apart: 25, of which 17 were waited for; matrix products, arithmetic and copies ran while one was open for 8% of the time, Pallas kernels for 0%

profile of v1, /device:TPU:0, one launch (start us, length us, event | category | flops | bytes accessed | tf_op | source)
XLA Modules:
  0.0 1595.0 jit_solution(7012503005836382189)
XLA Ops:
  9.5 43.1 %all_to_all.126 = bf16[6,197,384]{1,0,2:T(8,128)(2,1)S(1)} all-to-all(bf16[6,197,384]{1,0,2:T(8,128)(2,1)S(1)} %copy.107), channel_id=1, replica_groups=mesh['dp'=4,'row'=4,'col'=2] {'row'}, dimensions={2} | all-to-all | bytes 1815552 | tf_op jit(solution)/shard_map/all_to_all | solution.py:173
  62.7 17.6 %all-reduce.4 = (f32[24,197]{1,0:T(8,128)S(1)}, f32[24,197]{1,0:T(8,128)S(1)}) all-reduce(f32[24,197]{1,0:T(8,128)S(1)} %reduce_sum.178, f32[24,197]{1,0:T(8,128)S(1)} %reduce_sum.176), channel_id=1, replica_groups=mesh['dp'=4,'row'=4,'col'=2] {'row'}, use_global_device_ids=true, to_apply=%region_3.0 | all-reduce | flops 9456 | bytes 75648 | tf_op jit(solution)/shard_map/psum | solution.py:31
  82.6 9.3 all-gather.9.cloned.1.call-done
  91.9 4.9 all-to-all-start.1
  100.8 37.7 %collective-permute-done = bf16[96,576]{0,1:T(8,128)(2,1)S(1)} collective-permute-done((bf16[96,576]{0,1:T(8,128)(2,1)S(1)}, bf16[96,576]{0,1:T(8,128)(2,1)S(1)}, u32[]{:S(2)}, u32[]{:S(2)}) %collective-permute-start) | collective-permute-done | bytes 110624 | tf_op jit(solution)/shard_map/ppermute | solution.py:19
  142.9 15.0 collective-permute-done.1
  180.6 7.9 while.26
  191.4 81.2 %all_to_all.127 = bf16[6,197,384]{1,0,2:T(8,128)(2,1)} all-to-all(bf16[6,197,384]{1,0,2:T(8,128)(2,1)} %copy.119), channel_id=1, replica_groups=mesh['dp'=4,'row'=4,'col'=2] {'row'}, dimensions={2} | all-to-all | bytes 1815552 | tf_op jit(solution)/shard_map/all_to_all | solution.py:174
  282.5 24.3 %all-gather.11.cloned.1.call-done = bf16[48,197,192]{1,2,0:T(8,128)(2,1)} async-done(((bf16[12,197,192]{1,2,0:T(8,128)(2,1)}), bf16[48,197,192]{1,2,0:T(8,128)(2,1)}) %all-gather.11.cloned.1.call-update) | async-done | bytes 3631120 | tf_op jit(solution)/shard_map/all_gather | solution.py:68
  306.7 5.3 fusion.88
  312.1 6.3 all-gather.17.cloned.1.call-done
  323.3 11.0 reduce-scatter.5.cloned.1.call-done
  334.3 5.1 fusion.83
  339.4 48.0 %all-reduce.3 = (f32[24,197]{1,0:T(8,128)}, f32[24,197]{1,0:T(8,128)}) all-reduce(f32[24,197]{1,0:T(8,128)} %get-tuple-element.150, f32[24,197]{1,0:T(8,128)} %get-tuple-element.149), channel_id=1, replica_groups=mesh['dp'=4,'row'=4,'col'=2] {'row'}, use_global_device_ids=true, to_apply=%region_12.13 | all-reduce | flops 9456 | bytes 75648 | tf_op jit(solution)/shard_map/psum | solution.py:31
  392.0 11.2 all-gather.13.cloned.1.call-done
  403.2 4.9 all-to-all-start.2
  411.9 38.0 %collective-permute-done.3 = bf16[96,768]{1,0:T(8,128)(2,1)S(1)} collective-permute-done((bf16[96,768]{1,0:T(8,128)(2,1)}, bf16[96,768]{1,0:T(8,128)(2,1)S(1)}, u32[]{:S(2)}, u32[]{:S(2)}) %collective-permute-start.3) | collective-permute-done | bytes 147488 | tf_op jit(solution)/shard_map/ppermute | solution.py:19
  454.2 27.7 %all_gather.35 = bf16[768,384]{0,1:T(8,128)(2,1)} all-gather(bf16[768,96]{0,1:T(8,128)(2,1)} %bitcast.268), channel_id=1, replica_groups=mesh['dp'=4,'row'=4,'col'=2] {'row'}, dimensions={1}, use_global_device_ids=true | all-gather | bytes 737280 | tf_op jit(solution)/shard_map/all_gather | solution.py:88
  491.0 5.5 copy.122
  496.5 5.3 all_to_all.112
  501.8 5.5 copy.117
  507.2 5.3 all_to_all.100
  512.6 5.6 multiply_convert_fusion.1
  523.1 255.8 %all-gather.19.cloned.1.call-done = bf16[48,197,768]{2,1,0:T(8,128)(2,1)} async-done(((bf16[12,197,768]{2,1,0:T(8,128)(2,1)}), bf16[48,197,768]{2,1,0:T(8,128)(2,1)}) %all-gather.19.cloned.1.call-update) | async-done | bytes 14524432 | tf_op jit(solution)/shard_map/all_gather | solution.py:68
  778.9 9.5 fusion.77
  788.4 10.8 reduce-scatter.9.cloned.1.call-done
  803.4 20.8 %all-reduce.2 = (f32[24,197]{1,0:T(8,128)}, f32[24,197]{1,0:T(8,128)}) all-reduce(f32[24,197]{1,0:T(8,128)} %get-tuple-element.140, f32[24,197]{1,0:T(8,128)} %get-tuple-element.146), channel_id=1, replica_groups=mesh['dp'=4,'row'=4,'col'=2] {'row'}, use_global_device_ids=true, to_apply=%region_18.19 | all-reduce | flops 9456 | bytes 75648 | tf_op jit(solution)/shard_map/psum | solution.py:31
  830.3 9.3 all-gather.21.cloned.1.call-done
  839.6 4.9 all-to-all-start.6
  846.0 60.5 %all_gather.38 = bf16[192,384]{0,1:T(8,128)(2,1)} all-gather(bf16[192,96]{0,1:T(8,128)(2,1)} %copy.124), channel_id=1, replica_groups=mesh['dp'=4,'row'=4,'col'=2] {'row'}, dimensions={1}, use_global_device_ids=true | all-gather | bytes 184320 | tf_op jit(solution)/shard_map/all_gather | solution.py:88
  906.5 5.4 copy.123
  912.0 5.3 all_to_all.116
  924.2 17.8 %while.27 = (s32[]{:T(128)}, bf16[2,6,197,3,64]{2,4,3,1,0:T(8,128)(2,1)}, bf16[2,6,197,3,64]{2,4,3,1,0:T(8,128)(2,1)}, bf16[2,6,197,3,64]{2,4,3,1,0:T(8,128)(2,1...) while((s32[]{:T(128)}, ...), condition=%wide.region_21.22_spmd, body=%wide.region_19.21_spmd.sunk | while | flops 456593600 | bytes 55074784 | solution.py:238
  948.8 213.1 %all-gather.23.cloned.1.call-done = bf16[48,197,576]{2,1,0:T(8,128)(2,1)} async-done(((bf16[12,197,576]{2,1,0:T(8,128)(2,1)}), bf16[48,197,576]{2,1,0:T(8,128)(2,1)}) %all-gather.23.cloned.1.call-update) | async-done | bytes 10893328 | tf_op jit(solution)/shard_map/all_gather | solution.py:68
  1161.9 11.7 fusion.89
  1173.8 241.2 %all-gather.15.cloned.1.call-done = bf16[48,197,768]{2,1,0:T(8,128)(2,1)} async-done(((bf16[12,197,768]{2,1,0:T(8,128)(2,1)}), bf16[48,197,768]{2,1,0:T(8,128)(2,1)}) %all-gather.15.cloned.1.call-update) | async-done | bytes 14524432 | tf_op jit(solution)/shard_map/all_gather | solution.py:68
  1415.0 11.9 fusion.79
  1428.8 8.4 fusion.70
  1441.7 18.1 %all-reduce.1 = (f32[24,197]{1,0:T(8,128)}, f32[24,197]{1,0:T(8,128)}) all-reduce(f32[24,197]{1,0:T(8,128)} %get-tuple-element.142, f32[24,197]{1,0:T(8,128)} %get-tuple-element.145), channel_id=1, replica_groups=mesh['dp'=4,'row'=4,'col'=2] {'row'}, use_global_device_ids=true, to_apply=%region_26.27 | all-reduce | flops 9456 | bytes 75648 | tf_op jit(solution)/shard_map/psum | solution.py:31
  1462.6 7.5 add_convert_fusion.1
  1473.6 8.1 fusion.67
  1486.0 12.8 all-to-all-done.3
  1503.4 7.1 fusion.69
  1517.3 7.4 reduce_sum.191
  1525.8 6.6 reduce.5
  1532.5 10.0 all-reduce.5
  1544.7 17.3 %all-reduce.9.cloned.1.call-done = (bf16[3,96,256]{1,2,0:T(8,128)(2,1)}, bf16[96,768]{1,0:T(8,128)(2,1)}, bf16[96,768]{1,0:T(8,128)(2,1)}) async-done(((bf16[3,96,256]{1,2,0:T(8,128)(2,1)}, bf16[96,768]{1,0:T(8,128)(2,1)}, bf16[96,768]{1,0:T(8,128)(2,1)}), (bf16[3,96,256]{1,2,0:T(8,128)(2,1)}, bf16[96,768]{1,0:T(8,128)(2,1)}, bf16[96,768]{1,0:T(8,128)(2,1)})) %all-reduce.9.cloned.1.call-update) | async-done | bytes 442384 | tf_op jit(solution)/shard_map/psum | solution.py:117
  1567.1 12.6 all-reduce
  (253 shorter events, 186.1 us)
Async XLA Ops:
  7.2 84.7 %all-gather.9.cloned.1.call-start = ((), (), s32[]{:S(2)}) async-start(), calls=%async_computation.12 | async-start | bytes 3538944 | tf_op jit(solution)/shard_map/all_gather | solution.py:64
  55.3 4.4 copy-start.3
  59.7 21.2 %copy-start.34 = (f32[96]{0:T(128)S(1)}, f32[96]{0:T(128)}, u32[]{:S(2)}) copy-start(f32[96]{0:T(128)} %param.18) | copy-start | bytes 1156
  59.7 21.2 %copy-start.41 = (f32[96]{0:T(128)S(1)}, f32[96]{0:T(128)}, u32[]{:S(2)}) copy-start(f32[96]{0:T(128)} %param.19) | copy-start | bytes 1156
  62.7 19.8 %copy-start.1 = (f32[4,6,197,96]{2,3,1,0:T(8,128)}, f32[4,6,197,96]{2,3,1,0:T(8,128)S(1)}, u32[]{:S(2)}) copy-start(f32[4,6,197,96]{2,3,1,0:T(8,128)S(1)} %copy.109) | copy-start | bytes 5446660
  82.5 14.2 copy-start.27
  82.5 60.3 %copy-start.38 = (f32[2,192]{1,0:T(2,128)S(1)}, f32[2,192]{1,0:T(2,128)}, u32[]{:S(2)}) copy-start(f32[2,192]{1,0:T(2,128)} %param.21) | copy-start | bytes 4612
  91.9 73.9 %all-to-all-start.1 = ((bf16[48,197,96]{1,2,0:T(8,128)(2,1)}), bf16[48,197,96]{1,2,0:T(8,128)(2,1)S(1)}, u32[]{:S(2)}, u32[]{:S(2)}) async-start(bf16[48,197,96]{1,2,0:T(8,128)(2,1)} %all-gather.9.cloned.1.call-done), calls=%async_computation.1 | async-start | bytes 4718592 | tf_op jit(solution)/shard_map/all_to_all | solution.py:72
  96.7 210.0 %all-gather.11.cloned.1.call-start = ((), (), s32[]{:S(2)}) async-start(), calls=%async_computation.13 | async-start | bytes 5898240 | tf_op jit(solution)/shard_map/all_gather | solution.py:68
  96.9 68.9 %copy-start.16 = (bf16[96,3,3,64]{0,3,2,1:T(8,128)(2,1)}, bf16[96,3,3,64]{0,3,2,1:T(8,128)(2,1)S(1)}, u32[]{:S(2)}) copy-start(bf16[96,3,3,64]{0,3,2,1:T(8,128)(2,1)S(1)} %copy.114) | copy-start | bytes 331780
  96.9 41.5 %collective-permute-start = (bf16[96,576]{0,1:T(8,128)(2,1)S(1)}, bf16[96,576]{0,1:T(8,128)(2,1)S(1)}, u32[]{:S(2)}, u32[]{:S(2)}) collective-permute-start(bf16[96,576]{0,1:T(8,128)(2,1)S(1)} %bitcast.261), channel_id=1, source_target_pairs={{0,6},{2,0},{4,2},{6,4},{1,7},{3,1},{5,3},{7,5},{8,14},{10,8},{12,... | collective-permute-start | bytes 331784 | tf_op jit(solution)/shard_map/ppermute | solution.py:19
  138.5 19.4 %collective-permute-start.1 = (bf16[96,576]{0,1:T(8,128)(2,1)S(1)}, bf16[96,576]{0,1:T(8,128)(2,1)S(1)}, u32[]{:S(2)}, u32[]{:S(2)}) collective-permute-start(bf16[96,576]{0,1:T(8,128)(2,1)S(1)} %collective-permute-done), channel_id=1, source_target_pairs={{0,6},{2,0},{4,2},{6,4},{1,7},{3,1},{5,3},{7,5},{8,14},{10,8},{12,... | collective-permute-start | bytes 331784 | tf_op jit(solution)/shard_map/ppermute | solution.py:19
  157.9 5.4 collective-permute-start.2
  188.5 129.9 %all-gather.17.cloned.1.call-start = ((), (), s32[]{:S(2)}) async-start(), calls=%async_computation.18 | async-start | bytes 3538944 | tf_op jit(solution)/shard_map/all_gather | solution.py:64
  279.2 55.0 %reduce-scatter.5.cloned.1.call-start = ((), (), s32[]{:S(2)}) async-start(), calls=%async_computation.14 | async-start | bytes 7077888 | tf_op jit(solution)/shard_map/reduce_scatter | solution.py:78
  312.1 22.2 %copy-start.42 = (f32[96]{0:T(128)S(1)}, f32[96]{0:T(128)}, u32[]{:S(2)}) copy-start(f32[96]{0:T(128)} %param.22) | copy-start | bytes 1156
  318.3 73.6 %all-to-all-start.5 = ((bf16[48,197,96]{1,2,0:T(8,128)(2,1)}), bf16[48,197,96]{1,2,0:T(8,128)(2,1)}, u32[]{:S(2)}, u32[]{:S(2)}) async-start(bf16[48,197,96]{1,2,0:T(8,128)(2,1)} %all-gather.17.cloned.1.call-done), calls=%async_computation.7 | async-start | bytes 4718592 | tf_op jit(solution)/shard_map/all_to_all | solution.py:87
  323.2 65.5 %copy-start.33 = (f32[96]{0:T(128)S(1)}, f32[96]{0:T(128)}, u32[]{:S(2)}) copy-start(f32[96]{0:T(128)} %param.23) | copy-start | bytes 1156
  323.2 65.5 %copy-start.43 = (f32[96]{0:T(128)S(1)}, f32[96]{0:T(128)}, u32[]{:S(2)}) copy-start(f32[96]{0:T(128)} %param.24) | copy-start | bytes 1156
  323.2 80.0 %all-gather.13.cloned.1.call-start = ((), (), s32[]{:S(2)}) async-start(), calls=%async_computation.15 | async-start | bytes 3538944 | tf_op jit(solution)/shard_map/all_gather | solution.py:64
  403.2 98.6 %all-to-all-start.2 = ((bf16[48,197,96]{1,2,0:T(8,128)(2,1)}), bf16[48,197,96]{1,2,0:T(8,128)(2,1)}, u32[]{:S(2)}, u32[]{:S(2)}) async-start(bf16[48,197,96]{1,2,0:T(8,128)(2,1)} %all-gather.13.cloned.1.call-done), calls=%async_computation.3 | async-start | bytes 4718592 | tf_op jit(solution)/shard_map/all_to_all | solution.py:72
  408.1 370.8 %all-gather.19.cloned.1.call-start = ((), (), s32[]{:S(2)}) async-start(), calls=%async_computation.19 | async-start | bytes 18432000 | tf_op jit(solution)/shard_map/all_gather | solution.py:68
  408.1 41.8 %collective-permute-start.3 = (bf16[96,768]{1,0:T(8,128)(2,1)}, bf16[96,768]{1,0:T(8,128)(2,1)S(1)}, u32[]{:S(2)}, u32[]{:S(2)}) collective-permute-start(bf16[96,768]{1,0:T(8,128)(2,1)} %param.25), channel_id=1, source_target_pairs={{0,6},{2,0},{4,2},{6,4},{1,7},{3,1},{5,3},{7,5},{8,14},{10,8},{12,... | collective-permute-start | bytes 442376 | tf_op jit(solution)/shard_map/ppermute | solution.py:19
  449.9 32.8 %collective-permute-start.4 = (bf16[96,768]{1,0:T(8,128)(2,1)S(1)}, bf16[96,768]{1,0:T(8,128)(2,1)S(1)}, u32[]{:S(2)}, u32[]{:S(2)}) collective-permute-start(bf16[96,768]{1,0:T(8,128)(2,1)S(1)} %collective-permute-done.3), channel_id=1, source_target_pairs={{0,6},{2,0},{4,2},{6,4},{1,7},{3,1},{5,3},{7,5},{8,14},{10,8},{12,... | collective-permute-start | bytes 442376 | tf_op jit(solution)/shard_map/ppermute | solution.py:19
  482.8 6.2 collective-permute-start.5
  507.2 5.3 copy-start.44
  512.6 5.6 copy-start.18
  512.6 5.6 copy-start.22
  523.0 276.3 %reduce-scatter.9.cloned.1.call-start = ((), (), s32[]{:S(2)}) async-start(), calls=%async_computation.20 | async-start | bytes 7077888 | tf_op jit(solution)/shard_map/reduce_scatter | solution.py:95
  788.4 51.3 %all-gather.21.cloned.1.call-start = ((), (), s32[]{:S(2)}) async-start(), calls=%async_computation.21 | async-start | bytes 3538944 | tf_op jit(solution)/shard_map/all_gather | solution.py:64
  839.6 66.9 %all-to-all-start.6 = ((bf16[48,197,96]{1,2,0:T(8,128)(2,1)}), bf16[48,197,96]{1,2,0:T(8,128)(2,1)}, u32[]{:S(2)}, u32[]{:S(2)}) async-start(bf16[48,197,96]{1,2,0:T(8,128)(2,1)} %all-gather.21.cloned.1.call-done), calls=%async_computation.9 | async-start | bytes 4718592 | tf_op jit(solution)/shard_map/all_to_all | solution.py:87
  844.5 317.4 %all-gather.23.cloned.1.call-start = ((), (), s32[]{:S(2)}) async-start(), calls=%async_computation.22 | async-start | bytes 15360000 | tf_op jit(solution)/shard_map/all_gather | solution.py:68
  948.1 213.7 %copy-start.17 = (bf16[96,3,3,64]{0,3,2,1:T(8,128)(2,1)S(1)}, bf16[96,3,3,64]{0,3,2,1:T(8,128)(2,1)}, u32[]{:S(2)}) copy-start(bf16[96,3,3,64]{0,3,2,1:T(8,128)(2,1)} %copy-done.16) | copy-start | bytes 331780
  948.1 466.9 %all-gather.15.cloned.1.call-start = ((), (), s32[]{:S(2)}) async-start(), calls=%async_computation.16 | async-start | bytes 18432000 | tf_op jit(solution)/shard_map/all_gather | solution.py:68
  948.7 488.5 %reduce-scatter.11.cloned.1.call-start = ((), (), s32[]{:S(2)}) async-start(), calls=%async_computation.23 | async-start | bytes 7077888 | tf_op jit(solution)/shard_map/reduce_scatter | solution.py:95
  1173.5 241.5 %copy-start.23 = (bf16[96,768]{1,0:T(8,128)(2,1)S(1)}, bf16[96,768]{1,0:T(8,128)(2,1)}, u32[]{:S(2)}) copy-start(bf16[96,768]{1,0:T(8,128)(2,1)} %param.27) | copy-start | bytes 442372
  1173.6 289.0 %reduce-scatter.7.cloned.1.call-start = ((), (), s32[]{:S(2)}) async-start(), calls=%async_computation.17 | async-start | bytes 7077888 | tf_op jit(solution)/shard_map/reduce_scatter | solution.py:78
  1428.8 8.4 copy-start.35
  1437.2 25.4 %copy-start = (f32[24,197,96]{1,2,0:T(8,128)S(1)}, f32[24,197,96]{1,2,0:T(8,128)}, u32[]{:S(2)}) copy-start(f32[24,197,96]{1,2,0:T(8,128)} %get-tuple-element.202) | copy-start | bytes 5446660
  1437.2 25.4 %copy-start.5 = (bf16[4,6,197,96]{2,3,1,0:T(8,128)(2,1)S(1)}, bf16[4,6,197,96]{2,3,1,0:T(8,128)(2,1)}, u32[]{:S(2)}) copy-start(bf16[4,6,197,96]{2,3,1,0:T(8,128)(2,1)} %copy.121) | copy-start | bytes 2723332
  1470.0 28.8 %all-to-all-start.3 = ((bf16[24,197,96]{1,2,0:T(8,128)(2,1)}), bf16[24,197,96]{1,2,0:T(8,128)(2,1)S(1)}, u32[]{:S(2)}, u32[]{:S(2)}) async-start(bf16[24,197,96]{1,2,0:T(8,128)(2,1)} %get-tuple-element.211), calls=%async_computation.5 | async-start | bytes 2359296 | tf_op jit(solution)/shard_map/all_to_all | solution.py:271
  1473.6 8.1 copy-start.4
  1498.8 84.3 %all-to-all-start.7 = ((bf16[24,197,96]{1,2,0:T(8,128)(2,1)}), bf16[24,197,96]{1,2,0:T(8,128)(2,1)}, u32[]{:S(2)}, u32[]{:S(2)}) async-start(bf16[24,197,96]{1,2,0:T(8,128)(2,1)} %get-tuple-element.210), calls=%async_computation.11 | async-start | bytes 2359296 | tf_op jit(solution)/shard_map/all_to_all | solution.py:278
  1503.1 59.0 %all-reduce.9.cloned.1.call-start = ((), (), s32[]{:S(2)}) async-start(), calls=%async_computation.24 | async-start | bytes 983040 | tf_op jit(solution)/shard_map/psum | solution.py:117
  1525.8 6.7 copy-start.39
  1525.8 6.7 copy-start.40
  1525.8 41.3 %copy-start.36 = (f32[96]{0:T(128)S(1)}, f32[96]{0:T(128)}, u32[]{:S(2)}) copy-start(f32[96]{0:T(128)} %get-tuple-element.141) | copy-start | bytes 1156
  1525.8 41.3 %copy-start.37 = (f32[96]{0:T(128)S(1)}, f32[96]{0:T(128)}, u32[]{:S(2)}) copy-start(f32[96]{0:T(128)} %get-tuple-element.148) | copy-start | bytes 1156
  (33 other events, 38.8 us)
Sparse Core Ops, SparseCore 0:
  82.6 9.1 all-gather.8
  188.6 118.0 all-gather.10
  308.3 10.0 all-gather.16
  320.5 13.7 reduce-scatter.4
  392.1 11.0 all-gather.12
  523.1 255.6 all-gather.18
  788.5 10.7 reduce-scatter.8
  830.5 9.1 all-gather.20
  948.3 213.5 all-gather.22
  1163.3 251.7 all-gather.14
  1417.3 10.7 reduce-scatter.10
  1430.3 13.8 reduce-scatter.6
  1514.8 47.2 all-reduce.8
